TPU v7x, 32 devices: a whole 2x2x4 slice. The times are simulated.
32 devices in a mesh: groups: 2 (over y), tm: 8 (over z, x), space: 2 (over core).
Axes of the slice: x: 2, y: 2, z: 4, core: 2. Of those that a mesh axis runs over, the one named last changes fastest.
Arguments:
- iterate: float32 [16, 16, 16, 128], P(('groups', 'tm'), 'space'), parts along dimension 0, may hold values from -0.7 to 1.3
- source: float32 [16, 16, 16, 128], P(('groups', 'tm'), 'space'), parts along dimension 0, may hold values from -6 to 6
- diffusivity: float32 [32, 16, 128], P(('groups', 'space')), parts along dimension 0, may hold values from 0.1 to 1
Outputs:
- new_iterate: float32 [16, 16, 16, 128], P(('groups', 'tm'), 'space'), parts along dimension 0
- new_residual: float32 [16, 16, 16, 128], P(('groups', 'tm'), 'space'), parts along dimension 0
There are 2 independent parts, one for each index of `groups`. A program takes and returns all parts, laid end to end along the dimension named above; each array names one. Nothing has to cross between parts.
All inputs are finite; a program needn't handle non-finite values.
Results may differ from a plain program's by a relative error of at most 0.0019.
Values sent between devices are 32-bit elements; how exact they have to be, the bound alone decides.
A program may use at most 64 MiB of HBM per device.

v0:
```python
import math

import jax
import jax.numpy as jnp
from jax import lax
from jax.sharding import PartitionSpec as P

SWEEPS = 6


frac_order = 0.3
step_length = 0.01
gamma_factor = 0.9086387328532904


def with_halo(value, sides, width):
    for axis, dim in sides:
        peers, length = (lax.axis_size(axis), value.shape[dim])
        up = [(i, (i + 1) % peers) for i in range(peers - 1)]
        down = [(j, i) for i, j in up]
        last = lax.slice_in_dim(value, length - width, length, axis=dim)
        first = lax.slice_in_dim(value, 0, width, axis=dim)
        before = lax.ppermute(last, axis, up)
        after = lax.ppermute(first, axis, down)
        value = jnp.concatenate([before, value, after], axis=dim)
    return value


def history_weights(lags):
    scale = 1.0 / (step_length**frac_order * gamma_factor)
    power = 1.0 - frac_order
    safe = jnp.maximum(lags, 0.0)
    upper = (safe + 1.0) ** power - safe**power
    lower = jnp.where(safe >= 1.0, safe**power - jnp.maximum(safe - 1.0, 0.0) ** power, 0.0)
    return jnp.where(lags >= 0.0, (upper - lower) * scale, 0.0)


def circulant_spectrum(freqs, total):
    lags = jnp.arange(total, dtype=jnp.int32)
    first = jnp.where(lags < total // 2, history_weights(lags.astype(jnp.float32)), 0.0)
    phase = (freqs[:, None] * lags[None, :] % total).astype(jnp.float32) * (2.0 * math.pi / total)
    real_part = jnp.sum(first[None, :] * jnp.cos(phase), axis=1)
    imag_part = -jnp.sum(first[None, :] * jnp.sin(phase), axis=1)
    return (real_part, imag_part)


def fourier_tables(total):
    index = jnp.arange(total, dtype=jnp.int32)
    phase = (index[:, None] * index[None, :] % total).astype(jnp.float32) * (2.0 * math.pi / total)
    return (jnp.cos(phase), jnp.sin(phase))


def neighbour_sum(padded):
    inner = padded[..., 1:-1, :, :]
    result = padded[..., 2:, :, :] + padded[..., :-2, :, :]
    along_y = jnp.pad(inner, [(0, 0)] * (inner.ndim - 2) + [(1, 1), (0, 0)])
    result = result + along_y[..., 2:, :] + along_y[..., :-2, :]
    along_x = jnp.pad(inner, [(0, 0)] * (inner.ndim - 1) + [(1, 1)])
    return result + along_x[..., 2:] + along_x[..., :-2]


def jacobi_step(
    spec_re, spec_im, sol_re, sol_im, stiff_re, stiff_im, lam_re, lam_im, inv_re, inv_im
):
    res_re = spec_re - (lam_re * sol_re - lam_im * sol_im) - stiff_re
    res_im = spec_im - (lam_re * sol_im + lam_im * sol_re) - stiff_im
    return (
        sol_re + (res_re * inv_re - res_im * inv_im),
        sol_im + (res_re * inv_im + res_im * inv_re),
    )


def stiffness_pair(sol_re, sol_im, diffusivity):
    stacked = jnp.stack([sol_re, sol_im])
    padded = with_halo(stacked, (("space", 2),), 1)
    stiff = diffusivity * (6.0 * stacked - neighbour_sum(padded))
    return (stiff[0], stiff[1])


def time_product(matrix, field):
    return jnp.dot(matrix, field, precision=lax.Precision.HIGHEST)


def inner_products(residual, image):
    return lax.psum((jnp.sum(residual * image), jnp.sum(image * image)), ("tm", "space"))


def on_device(iterate, source, diffusivity):
    steps_here = iterate.shape[0]
    slab_shape = iterate.shape
    cells = slab_shape[1] * slab_shape[2] * slab_shape[3]
    total = steps_here * lax.axis_size("tm")
    my_times = lax.axis_index("tm") * steps_here + jnp.arange(steps_here, dtype=jnp.int32)
    times = jnp.arange(total, dtype=jnp.int32)
    toeplitz = history_weights((times[:, None] - times[None, :]).astype(jnp.float32))
    cos_table, sin_table = fourier_tables(total)
    padded = with_halo(iterate, (("space", 1),), 1)
    stiff_iter = diffusivity * (6.0 * iterate - neighbour_sum(padded))
    flat_iter = iterate.reshape(steps_here, cells)
    flat_source = source.reshape(steps_here, cells)
    flat_stiff = stiff_iter.reshape(steps_here, cells)
    iter_cols, source_cols, stiff_cols = (
        lax.all_to_all(flat_iter, "tm", split_axis=1, concat_axis=0, tiled=True),
        lax.all_to_all(flat_source, "tm", split_axis=1, concat_axis=0, tiled=True),
        lax.all_to_all(flat_stiff, "tm", split_axis=1, concat_axis=0, tiled=True),
    )
    residual = source_cols - time_product(toeplitz, iter_cols) - stiff_cols
    spec_re = time_product(cos_table, residual)
    spec_im = -time_product(sin_table, residual)
    spec_re, spec_im = (
        lax.all_to_all(spec_re, "tm", split_axis=0, concat_axis=1, tiled=True),
        lax.all_to_all(spec_im, "tm", split_axis=0, concat_axis=1, tiled=True),
    )
    spec_re = spec_re.reshape(slab_shape)
    spec_im = spec_im.reshape(slab_shape)
    lam_re, lam_im = circulant_spectrum(my_times, total)
    lam_re = lam_re[:, None, None, None]
    lam_im = lam_im[:, None, None, None]
    diag_re = lam_re + 6.0 * diffusivity
    denom = diag_re * diag_re + lam_im * lam_im
    inv_re = diag_re / denom
    inv_im = -lam_im / denom
    sol_re = spec_re * inv_re - spec_im * inv_im
    sol_im = spec_re * inv_im + spec_im * inv_re
    for sweep in range(SWEEPS - 1):
        stiff_re, stiff_im = stiffness_pair(sol_re, sol_im, diffusivity)
        sol_re, sol_im = jacobi_step(
            spec_re, spec_im, sol_re, sol_im, stiff_re, stiff_im, lam_re, lam_im, inv_re, inv_im
        )
    stiff_re, stiff_im = stiffness_pair(sol_re, sol_im, diffusivity)
    sol_re, sol_im, stiff_re, stiff_im = (
        lax.all_to_all(
            sol_re.reshape(steps_here, cells), "tm", split_axis=1, concat_axis=0, tiled=True
        ),
        lax.all_to_all(
            sol_im.reshape(steps_here, cells), "tm", split_axis=1, concat_axis=0, tiled=True
        ),
        lax.all_to_all(
            stiff_re.reshape(steps_here, cells), "tm", split_axis=1, concat_axis=0, tiled=True
        ),
        lax.all_to_all(
            stiff_im.reshape(steps_here, cells), "tm", split_axis=1, concat_axis=0, tiled=True
        ),
    )
    correction = (time_product(cos_table, sol_re) - time_product(sin_table, sol_im)) / total
    stiff_time = (time_product(cos_table, stiff_re) - time_product(sin_table, stiff_im)) / total
    image = time_product(toeplitz, correction) + stiff_time
    inner_ri, inner_ii = inner_products(residual, image)
    step = inner_ri / inner_ii
    new_residual = residual - step * image
    correction_slab, residual_back = (
        lax.all_to_all(correction, "tm", split_axis=0, concat_axis=1, tiled=True),
        lax.all_to_all(new_residual, "tm", split_axis=0, concat_axis=1, tiled=True),
    )
    new_iterate = iterate + step * correction_slab.reshape(slab_shape)
    return (new_iterate, residual_back.reshape(slab_shape))


def solution(mesh):
    in_specs = (
        P(("groups", "tm"), "space", None, None),
        P(("groups", "tm"), "space", None, None),
        P(("groups", "space"), None, None),
    )
    out_specs = (P(("groups", "tm"), "space", None, None), P(("groups", "tm"), "space", None, None))
    return jax.shard_map(
        on_device, mesh=mesh, in_specs=in_specs, out_specs=out_specs, check_vma=False
    )
```

profile of v0, /device:TPU:0, one launch (start us, length us, event | category | flops | bytes accessed | tf_op | source)
XLA Modules:
  0.0 186.0 jit_solution(9967362061430937001)
XLA Ops:
  0.6 7.3 %all-to-all-start = ((f32[1,8,2048]{2,0,1:T(1,128)}), f32[1,8,2048]{2,0,1:T(1,128)S(1)}, u32[]{:S(2)}, u32[]{:S(2)}) async-start(f32[1,8,2048]{2,0,1:T(1,128)} %bitcast.201), calls=%async_computation | async-start | bytes 131072 | tf_op jit(solution)/shard_map/all_to_all | solution.py:104
  8.6 1.3 collective-permute-start
  9.9 3.0 %collective-permute-start.1 = (f32[1,1,16,128]{3,2,1,0:T(8,128)S(1)}, f32[1,1,16,128]{3,2,1,0:T(8,128)S(1)}, u32[]{:S(2)}, u32[]{:S(2)}) collective-permute-start(f32[1,1,16,128]{3,2,1,0:T(8,128)S(1)} %get-tuple-element.35), channel_id=1, source_target_pairs={{0,1},{2,3},{4,5},{6,7},{8,9},{10,11},{12,13},{14,15},{16,17},{18,... | collective-permute-start | bytes 24584 | tf_op jit(solution)/shard_map/ppermute | solution.py:23
  13.0 1.9 %all-to-all-done = f32[1,8,2048]{2,0,1:T(1,128)S(1)} async-done(((f32[1,8,2048]{2,0,1:T(1,128)}), f32[1,8,2048]{2,0,1:T(1,128)S(1)}, u32[]{:S(2)}, u32[]{:S(2)}) %all-to-all-start) | async-done | bytes 65568 | tf_op jit(solution)/shard_map/all_to_all | solution.py:104
  14.8 4.3 %all-to-all-start.1 = ((f32[1,8,2048]{2,0,1:T(1,128)}), f32[1,8,2048]{2,0,1:T(1,128)S(1)}, u32[]{:S(2)}, u32[]{:S(2)}) async-start(f32[1,8,2048]{2,0,1:T(1,128)} %bitcast.1), calls=%async_computation.1 | async-start | bytes 131072 | tf_op jit(solution)/shard_map/all_to_all | solution.py:103
  19.2 1.3 fusion.52
  20.4 5.6 %all-to-all-done.1 = f32[1,8,2048]{2,0,1:T(1,128)S(1)} async-done(((f32[1,8,2048]{2,0,1:T(1,128)}), f32[1,8,2048]{2,0,1:T(1,128)S(1)}, u32[]{:S(2)}, u32[]{:S(2)}) %all-to-all-start.1) | async-done | bytes 65568 | tf_op jit(solution)/shard_map/all_to_all | solution.py:103
  26.0 9.3 %all_to_all.164 = f32[1,8,2048]{2,0,1:T(1,128)S(1)} all-to-all(f32[1,8,2048]{2,0,1:T(1,128)S(1)} %bitcast.200), channel_id=1, replica_groups=mesh['groups'=2,'tm'=8,'space'=2] {'tm'}, dimensions={1} | all-to-all | bytes 131072 | tf_op jit(solution)/shard_map/all_to_all | solution.py:105
  36.5 3.4 %all-to-all-start.4 = ((f32[8,1,2048]{2,1,0:T(1,128)}), f32[8,1,2048]{2,1,0:T(1,128)S(1)}, u32[]{:S(2)}, u32[]{:S(2)}) async-start(f32[8,1,2048]{2,1,0:T(1,128)} %copy.22), calls=%async_computation.4 | async-start | bytes 131072 | tf_op jit(solution)/shard_map/all_to_all | solution.py:112
  40.8 5.9 %all-to-all-done.4 = f32[8,1,2048]{2,1,0:T(1,128)S(1)} async-done(((f32[8,1,2048]{2,1,0:T(1,128)}), f32[8,1,2048]{2,1,0:T(1,128)S(1)}, u32[]{:S(2)}, u32[]{:S(2)}) %all-to-all-start.4) | async-done | bytes 65568 | tf_op jit(solution)/shard_map/all_to_all | solution.py:112
  46.7 3.4 %all-to-all-start.3 = ((f32[8,1,2048]{2,1,0:T(1,128)}), f32[8,1,2048]{2,1,0:T(1,128)S(1)}, u32[]{:S(2)}, u32[]{:S(2)}) async-start(f32[8,1,2048]{2,1,0:T(1,128)} %copy.21), calls=%async_computation.3 | async-start | bytes 131072 | tf_op jit(solution)/shard_map/all_to_all | solution.py:111
  52.8 4.1 %all-to-all-done.3 = f32[8,1,2048]{2,1,0:T(1,128)S(1)} async-done(((f32[8,1,2048]{2,1,0:T(1,128)}), f32[8,1,2048]{2,1,0:T(1,128)S(1)}, u32[]{:S(2)}, u32[]{:S(2)}) %all-to-all-start.3) | async-done | bytes 65568 | tf_op jit(solution)/shard_map/all_to_all | solution.py:111
  56.9 1.3 fusion.90
  58.2 1.3 collective-permute-start.2
  59.5 3.0 %collective-permute-start.3 = (f32[2,1,1,16,128]{4,3,2,1,0:T(8,128)S(1)}, f32[2,1,1,16,128]{4,3,2,1,0:T(8,128)S(1)}, u32[]{:S(2)}, u32[]{:S(2)}) collective-permute-start(f32[2,1,1,16,128]{4,3,2,1,0:T(8,128)S(1)} %get-tuple-element.33), channel_id=1, source_target_pairs={{0,1},{2,3},{4,5},{6,7},{8,9},{10,11},{12,13},{14,15},{16,17},{18,... | collective-permute-start | bytes 49160 | tf_op jit(solution)/shard_map/ppermute | solution.py:23
  62.5 0.8 collective-permute-done.3
  63.5 1.3 subtract_add_fusion.4
  64.8 1.3 collective-permute-start.4
  66.1 3.0 %collective-permute-start.5 = (f32[2,1,1,16,128]{4,3,2,1,0:T(8,128)S(1)}, f32[2,1,1,16,128]{4,3,2,1,0:T(8,128)S(1)}, u32[]{:S(2)}, u32[]{:S(2)}) collective-permute-start(f32[2,1,1,16,128]{4,3,2,1,0:T(8,128)S(1)} %get-tuple-element.31), channel_id=1, source_target_pairs={{0,1},{2,3},{4,5},{6,7},{8,9},{10,11},{12,13},{14,15},{16,17},{18,... | collective-permute-start | bytes 49160 | tf_op jit(solution)/shard_map/ppermute | solution.py:23
  69.2 0.8 collective-permute-done.5
  70.1 1.3 subtract_add_fusion.3
  71.4 1.3 collective-permute-start.6
  72.7 3.0 %collective-permute-start.7 = (f32[2,1,1,16,128]{4,3,2,1,0:T(8,128)S(1)}, f32[2,1,1,16,128]{4,3,2,1,0:T(8,128)S(1)}, u32[]{:S(2)}, u32[]{:S(2)}) collective-permute-start(f32[2,1,1,16,128]{4,3,2,1,0:T(8,128)S(1)} %get-tuple-element.29), channel_id=1, source_target_pairs={{0,1},{2,3},{4,5},{6,7},{8,9},{10,11},{12,13},{14,15},{16,17},{18,... | collective-permute-start | bytes 49160 | tf_op jit(solution)/shard_map/ppermute | solution.py:23
  76.7 1.3 fusion.92
  78.1 1.3 collective-permute-start.8
  79.4 3.0 %collective-permute-start.9 = (f32[2,1,1,16,128]{4,3,2,1,0:T(8,128)S(1)}, f32[2,1,1,16,128]{4,3,2,1,0:T(8,128)S(1)}, u32[]{:S(2)}, u32[]{:S(2)}) collective-permute-start(f32[2,1,1,16,128]{4,3,2,1,0:T(8,128)S(1)} %get-tuple-element.27), channel_id=1, source_target_pairs={{0,1},{2,3},{4,5},{6,7},{8,9},{10,11},{12,13},{14,15},{16,17},{18,... | collective-permute-start | bytes 49160 | tf_op jit(solution)/shard_map/ppermute | solution.py:23
  83.4 1.3 add_add_fusion.1
  84.7 1.3 collective-permute-start.10
  86.0 3.0 %collective-permute-start.11 = (f32[2,1,1,16,128]{4,3,2,1,0:T(8,128)S(1)}, f32[2,1,1,16,128]{4,3,2,1,0:T(8,128)S(1)}, u32[]{:S(2)}, u32[]{:S(2)}) collective-permute-start(f32[2,1,1,16,128]{4,3,2,1,0:T(8,128)S(1)} %get-tuple-element.25), channel_id=1, source_target_pairs={{0,1},{2,3},{4,5},{6,7},{8,9},{10,11},{12,13},{14,15},{16,17},{18,... | collective-permute-start | bytes 49160 | tf_op jit(solution)/shard_map/ppermute | solution.py:23
  90.0 2.0 %add_add_fusion = (f32[8,16,128]{2,1,0:T(8,128)}, f32[8,16,128]{2,1,0:T(8,128)}) fusion(f32[8,16,128]{2,1,0:T(8,128)S(1)} %get-tuple-element.8, f32[2,1,8,16,128]{4,3,2,1,0:T(8,128)S(1)} %fusion.34, f32[8,16,128]{2,1,0:T(8,128)S(1)} %bitcast.177, f32[]{:T(128)S(6)} %neg.11, f32[8,16,128]{2,1,0:T(8,128)S(1)} %get-tuple-element.9, f32[]{:T(128)} %get-tuple-element.38, ...), kind=kLoop, calls=%fused_computation.178 | loop fusion | flops 393216 | bytes 589840 | tf_op jit(solution)/shard_map/add | solution.py:69
  92.7 1.3 collective-permute-start.12
  94.0 3.0 %collective-permute-start.13 = (f32[2,1,1,16,128]{4,3,2,1,0:T(8,128)S(1)}, f32[2,1,1,16,128]{4,3,2,1,0:T(8,128)S(1)}, u32[]{:S(2)}, u32[]{:S(2)}) collective-permute-start(f32[2,1,1,16,128]{4,3,2,1,0:T(8,128)S(1)} %get-tuple-element.23), channel_id=1, source_target_pairs={{0,1},{2,3},{4,5},{6,7},{8,9},{10,11},{12,13},{14,15},{16,17},{18,... | collective-permute-start | bytes 49160 | tf_op jit(solution)/shard_map/ppermute | solution.py:23
  97.0 0.9 pad_maximum_fusion.5
  97.9 3.4 %all-to-all-start.5 = ((f32[1,8,2048]{2,0,1:T(1,128)}), f32[1,8,2048]{2,0,1:T(1,128)S(1)}, u32[]{:S(2)}, u32[]{:S(2)}) async-start(f32[1,8,2048]{2,0,1:T(1,128)} %bitcast.28), calls=%async_computation.5 | async-start | bytes 131072 | tf_op jit(solution)/shard_map/all_to_all | solution.py:132
  101.3 1.1 fusion.40
  103.1 5.1 %all-to-all-done.5 = f32[1,8,2048]{2,0,1:T(1,128)S(1)} async-done(((f32[1,8,2048]{2,0,1:T(1,128)}), f32[1,8,2048]{2,0,1:T(1,128)S(1)}, u32[]{:S(2)}, u32[]{:S(2)}) %all-to-all-start.5) | async-done | bytes 65568 | tf_op jit(solution)/shard_map/all_to_all | solution.py:132
  108.1 3.4 %all-to-all-start.6 = ((f32[1,8,2048]{2,0,1:T(1,128)}), f32[1,8,2048]{2,0,1:T(1,128)S(1)}, u32[]{:S(2)}, u32[]{:S(2)}) async-start(f32[1,8,2048]{2,0,1:T(1,128)} %bitcast.29), calls=%async_computation.6 | async-start | bytes 131072 | tf_op jit(solution)/shard_map/all_to_all | solution.py:135
  111.8 6.6 %all-to-all-done.6 = f32[1,8,2048]{2,0,1:T(1,128)S(1)} async-done(((f32[1,8,2048]{2,0,1:T(1,128)}), f32[1,8,2048]{2,0,1:T(1,128)S(1)}, u32[]{:S(2)}, u32[]{:S(2)}) %all-to-all-start.6) | async-done | bytes 65568 | tf_op jit(solution)/shard_map/all_to_all | solution.py:135
  118.3 3.3 %all-to-all-start.7 = ((f32[1,8,2048]{2,0,1:T(1,128)}), f32[1,8,2048]{2,0,1:T(1,128)S(1)}, u32[]{:S(2)}, u32[]{:S(2)}) async-start(f32[1,8,2048]{2,0,1:T(1,128)} %bitcast.32), calls=%async_computation.7 | async-start | bytes 131072 | tf_op jit(solution)/shard_map/all_to_all | solution.py:138
  122.9 5.7 %all-to-all-done.7 = f32[1,8,2048]{2,0,1:T(1,128)S(1)} async-done(((f32[1,8,2048]{2,0,1:T(1,128)}), f32[1,8,2048]{2,0,1:T(1,128)S(1)}, u32[]{:S(2)}, u32[]{:S(2)}) %all-to-all-start.7) | async-done | bytes 65568 | tf_op jit(solution)/shard_map/all_to_all | solution.py:138
  128.5 3.3 %all-to-all-start.8 = ((f32[1,8,2048]{2,0,1:T(1,128)}), f32[1,8,2048]{2,0,1:T(1,128)S(1)}, u32[]{:S(2)}, u32[]{:S(2)}) async-start(f32[1,8,2048]{2,0,1:T(1,128)} %bitcast.33), calls=%async_computation.8 | async-start | bytes 131072 | tf_op jit(solution)/shard_map/all_to_all | solution.py:141
  132.2 6.6 %all-to-all-done.8 = f32[1,8,2048]{2,0,1:T(1,128)S(1)} async-done(((f32[1,8,2048]{2,0,1:T(1,128)}), f32[1,8,2048]{2,0,1:T(1,128)S(1)}, u32[]{:S(2)}, u32[]{:S(2)}) %all-to-all-start.8) | async-done | bytes 65568 | tf_op jit(solution)/shard_map/all_to_all | solution.py:141
  138.7 3.4 %all-to-all-start.9 = ((f32[8,1,2048]{2,1,0:T(1,128)}), f32[8,1,2048]{2,1,0:T(1,128)S(1)}, u32[]{:S(2)}, u32[]{:S(2)}) async-start(f32[8,1,2048]{2,1,0:T(1,128)} %copy.23), calls=%async_computation.9 | async-start | bytes 131072 | tf_op jit(solution)/shard_map/all_to_all | solution.py:152
  142.1 0.9 multiply_reduce_fusion
  143.0 30.1 %all-reduce.14 = (f32[]{:T(128)}, f32[]{:T(128)}) all-reduce(f32[]{:T(128)} %get-tuple-element.5, f32[]{:T(128)} %get-tuple-element.4), channel_id=1, replica_groups=mesh['groups'=2,'tm'=8,'space'=2] {'tm','space'}, use_global_device_ids=true, to_apply=%region_3.4 | all-reduce | flops 2 | bytes 16 | tf_op jit(solution)/shard_map/psum | solution.py:85
  175.1 3.4 %all-to-all-start.10 = ((f32[8,1,2048]{2,1,0:T(1,128)}), f32[8,1,2048]{2,1,0:T(1,128)S(1)}, u32[]{:S(2)}, u32[]{:S(2)}) async-start(f32[8,1,2048]{2,1,0:T(1,128)} %copy.24), calls=%async_computation.10 | async-start | bytes 131072 | tf_op jit(solution)/shard_map/all_to_all | solution.py:153
  178.5 1.5 add.357
  180.0 5.3 %all-to-all-done.10 = f32[8,1,2048]{2,1,0:T(1,128)S(1)} async-done(((f32[8,1,2048]{2,1,0:T(1,128)}), f32[8,1,2048]{2,1,0:T(1,128)S(1)}, u32[]{:S(2)}, u32[]{:S(2)}) %all-to-all-start.10) | async-done | bytes 65568 | tf_op jit(solution)/shard_map/all_to_all | solution.py:153
  (48 shorter events, 11.1 us)
Async XLA Ops:
  0.6 14.2 %all-to-all-start = ((f32[1,8,2048]{2,0,1:T(1,128)}), f32[1,8,2048]{2,0,1:T(1,128)S(1)}, u32[]{:S(2)}, u32[]{:S(2)}) async-start(f32[1,8,2048]{2,0,1:T(1,128)} %bitcast.201), calls=%async_computation | async-start | bytes 131072 | tf_op jit(solution)/shard_map/all_to_all | solution.py:104
  8.6 10.5 %collective-permute-start = (f32[1,1,16,128]{3,2,1,0:T(8,128)S(1)}, f32[1,1,16,128]{3,2,1,0:T(8,128)S(1)}, u32[]{:S(2)}, u32[]{:S(2)}) collective-permute-start(f32[1,1,16,128]{3,2,1,0:T(8,128)S(1)} %get-tuple-element.34), channel_id=1, source_target_pairs={{1,0},{3,2},{5,4},{7,6},{9,8},{11,10},{13,12},{15,14},{17,16},{19,... | collective-permute-start | bytes 24584 | tf_op jit(solution)/shard_map/ppermute | solution.py:24
  9.9 9.2 %collective-permute-start.1 = (f32[1,1,16,128]{3,2,1,0:T(8,128)S(1)}, f32[1,1,16,128]{3,2,1,0:T(8,128)S(1)}, u32[]{:S(2)}, u32[]{:S(2)}) collective-permute-start(f32[1,1,16,128]{3,2,1,0:T(8,128)S(1)} %get-tuple-element.35), channel_id=1, source_target_pairs={{0,1},{2,3},{4,5},{6,7},{8,9},{10,11},{12,13},{14,15},{16,17},{18,... | collective-permute-start | bytes 24584 | tf_op jit(solution)/shard_map/ppermute | solution.py:23
  14.8 4.3 %copy-start = (f32[8,16,128]{2,1,0:T(8,128)S(1)}, f32[8,16,128]{2,1,0:T(8,128)}, u32[]{:S(2)}) copy-start(f32[8,16,128]{2,1,0:T(8,128)} %param.5) | copy-start | bytes 196612
  14.8 11.2 %all-to-all-start.1 = ((f32[1,8,2048]{2,0,1:T(1,128)}), f32[1,8,2048]{2,0,1:T(1,128)S(1)}, u32[]{:S(2)}, u32[]{:S(2)}) async-start(f32[1,8,2048]{2,0,1:T(1,128)} %bitcast.1), calls=%async_computation.1 | async-start | bytes 131072 | tf_op jit(solution)/shard_map/all_to_all | solution.py:103
  36.5 10.2 %all-to-all-start.4 = ((f32[8,1,2048]{2,1,0:T(1,128)}), f32[8,1,2048]{2,1,0:T(1,128)S(1)}, u32[]{:S(2)}, u32[]{:S(2)}) async-start(f32[8,1,2048]{2,1,0:T(1,128)} %copy.22), calls=%async_computation.4 | async-start | bytes 131072 | tf_op jit(solution)/shard_map/all_to_all | solution.py:112
  46.7 10.2 %all-to-all-start.3 = ((f32[8,1,2048]{2,1,0:T(1,128)}), f32[8,1,2048]{2,1,0:T(1,128)S(1)}, u32[]{:S(2)}, u32[]{:S(2)}) async-start(f32[8,1,2048]{2,1,0:T(1,128)} %copy.21), calls=%async_computation.3 | async-start | bytes 131072 | tf_op jit(solution)/shard_map/all_to_all | solution.py:111
  58.2 4.4 %collective-permute-start.2 = (f32[2,1,1,16,128]{4,3,2,1,0:T(8,128)S(1)}, f32[2,1,1,16,128]{4,3,2,1,0:T(8,128)S(1)}, u32[]{:S(2)}, u32[]{:S(2)}) collective-permute-start(f32[2,1,1,16,128]{4,3,2,1,0:T(8,128)S(1)} %get-tuple-element.32), channel_id=1, source_target_pairs={{1,0},{3,2},{5,4},{7,6},{9,8},{11,10},{13,12},{15,14},{17,16},{19,... | collective-permute-start | bytes 49160 | tf_op jit(solution)/shard_map/ppermute | solution.py:24
  59.5 3.9 %collective-permute-start.3 = (f32[2,1,1,16,128]{4,3,2,1,0:T(8,128)S(1)}, f32[2,1,1,16,128]{4,3,2,1,0:T(8,128)S(1)}, u32[]{:S(2)}, u32[]{:S(2)}) collective-permute-start(f32[2,1,1,16,128]{4,3,2,1,0:T(8,128)S(1)} %get-tuple-element.33), channel_id=1, source_target_pairs={{0,1},{2,3},{4,5},{6,7},{8,9},{10,11},{12,13},{14,15},{16,17},{18,... | collective-permute-start | bytes 49160 | tf_op jit(solution)/shard_map/ppermute | solution.py:23
  64.8 4.4 %collective-permute-start.4 = (f32[2,1,1,16,128]{4,3,2,1,0:T(8,128)S(1)}, f32[2,1,1,16,128]{4,3,2,1,0:T(8,128)S(1)}, u32[]{:S(2)}, u32[]{:S(2)}) collective-permute-start(f32[2,1,1,16,128]{4,3,2,1,0:T(8,128)S(1)} %get-tuple-element.30), channel_id=1, source_target_pairs={{1,0},{3,2},{5,4},{7,6},{9,8},{11,10},{13,12},{15,14},{17,16},{19,... | collective-permute-start | bytes 49160 | tf_op jit(solution)/shard_map/ppermute | solution.py:24
  66.1 3.9 %collective-permute-start.5 = (f32[2,1,1,16,128]{4,3,2,1,0:T(8,128)S(1)}, f32[2,1,1,16,128]{4,3,2,1,0:T(8,128)S(1)}, u32[]{:S(2)}, u32[]{:S(2)}) collective-permute-start(f32[2,1,1,16,128]{4,3,2,1,0:T(8,128)S(1)} %get-tuple-element.31), channel_id=1, source_target_pairs={{0,1},{2,3},{4,5},{6,7},{8,9},{10,11},{12,13},{14,15},{16,17},{18,... | collective-permute-start | bytes 49160 | tf_op jit(solution)/shard_map/ppermute | solution.py:23
  71.4 4.4 %collective-permute-start.6 = (f32[2,1,1,16,128]{4,3,2,1,0:T(8,128)S(1)}, f32[2,1,1,16,128]{4,3,2,1,0:T(8,128)S(1)}, u32[]{:S(2)}, u32[]{:S(2)}) collective-permute-start(f32[2,1,1,16,128]{4,3,2,1,0:T(8,128)S(1)} %get-tuple-element.28), channel_id=1, source_target_pairs={{1,0},{3,2},{5,4},{7,6},{9,8},{11,10},{13,12},{15,14},{17,16},{19,... | collective-permute-start | bytes 49160 | tf_op jit(solution)/shard_map/ppermute | solution.py:24
  72.7 3.9 %collective-permute-start.7 = (f32[2,1,1,16,128]{4,3,2,1,0:T(8,128)S(1)}, f32[2,1,1,16,128]{4,3,2,1,0:T(8,128)S(1)}, u32[]{:S(2)}, u32[]{:S(2)}) collective-permute-start(f32[2,1,1,16,128]{4,3,2,1,0:T(8,128)S(1)} %get-tuple-element.29), channel_id=1, source_target_pairs={{0,1},{2,3},{4,5},{6,7},{8,9},{10,11},{12,13},{14,15},{16,17},{18,... | collective-permute-start | bytes 49160 | tf_op jit(solution)/shard_map/ppermute | solution.py:23
  78.1 4.4 %collective-permute-start.8 = (f32[2,1,1,16,128]{4,3,2,1,0:T(8,128)S(1)}, f32[2,1,1,16,128]{4,3,2,1,0:T(8,128)S(1)}, u32[]{:S(2)}, u32[]{:S(2)}) collective-permute-start(f32[2,1,1,16,128]{4,3,2,1,0:T(8,128)S(1)} %get-tuple-element.26), channel_id=1, source_target_pairs={{1,0},{3,2},{5,4},{7,6},{9,8},{11,10},{13,12},{15,14},{17,16},{19,... | collective-permute-start | bytes 49160 | tf_op jit(solution)/shard_map/ppermute | solution.py:24
  79.4 3.9 %collective-permute-start.9 = (f32[2,1,1,16,128]{4,3,2,1,0:T(8,128)S(1)}, f32[2,1,1,16,128]{4,3,2,1,0:T(8,128)S(1)}, u32[]{:S(2)}, u32[]{:S(2)}) collective-permute-start(f32[2,1,1,16,128]{4,3,2,1,0:T(8,128)S(1)} %get-tuple-element.27), channel_id=1, source_target_pairs={{0,1},{2,3},{4,5},{6,7},{8,9},{10,11},{12,13},{14,15},{16,17},{18,... | collective-permute-start | bytes 49160 | tf_op jit(solution)/shard_map/ppermute | solution.py:23
  84.7 4.4 %collective-permute-start.10 = (f32[2,1,1,16,128]{4,3,2,1,0:T(8,128)S(1)}, f32[2,1,1,16,128]{4,3,2,1,0:T(8,128)S(1)}, u32[]{:S(2)}, u32[]{:S(2)}) collective-permute-start(f32[2,1,1,16,128]{4,3,2,1,0:T(8,128)S(1)} %get-tuple-element.24), channel_id=1, source_target_pairs={{1,0},{3,2},{5,4},{7,6},{9,8},{11,10},{13,12},{15,14},{17,16},{19,... | collective-permute-start | bytes 49160 | tf_op jit(solution)/shard_map/ppermute | solution.py:24
  86.0 3.9 %collective-permute-start.11 = (f32[2,1,1,16,128]{4,3,2,1,0:T(8,128)S(1)}, f32[2,1,1,16,128]{4,3,2,1,0:T(8,128)S(1)}, u32[]{:S(2)}, u32[]{:S(2)}) collective-permute-start(f32[2,1,1,16,128]{4,3,2,1,0:T(8,128)S(1)} %get-tuple-element.25), channel_id=1, source_target_pairs={{0,1},{2,3},{4,5},{6,7},{8,9},{10,11},{12,13},{14,15},{16,17},{18,... | collective-permute-start | bytes 49160 | tf_op jit(solution)/shard_map/ppermute | solution.py:23
  92.7 8.6 %collective-permute-start.12 = (f32[2,1,1,16,128]{4,3,2,1,0:T(8,128)S(1)}, f32[2,1,1,16,128]{4,3,2,1,0:T(8,128)S(1)}, u32[]{:S(2)}, u32[]{:S(2)}) collective-permute-start(f32[2,1,1,16,128]{4,3,2,1,0:T(8,128)S(1)} %get-tuple-element.22), channel_id=1, source_target_pairs={{1,0},{3,2},{5,4},{7,6},{9,8},{11,10},{13,12},{15,14},{17,16},{19,... | collective-permute-start | bytes 49160 | tf_op jit(solution)/shard_map/ppermute | solution.py:24
  94.0 7.3 %collective-permute-start.13 = (f32[2,1,1,16,128]{4,3,2,1,0:T(8,128)S(1)}, f32[2,1,1,16,128]{4,3,2,1,0:T(8,128)S(1)}, u32[]{:S(2)}, u32[]{:S(2)}) collective-permute-start(f32[2,1,1,16,128]{4,3,2,1,0:T(8,128)S(1)} %get-tuple-element.23), channel_id=1, source_target_pairs={{0,1},{2,3},{4,5},{6,7},{8,9},{10,11},{12,13},{14,15},{16,17},{18,... | collective-permute-start | bytes 49160 | tf_op jit(solution)/shard_map/ppermute | solution.py:23
  97.9 10.2 %all-to-all-start.5 = ((f32[1,8,2048]{2,0,1:T(1,128)}), f32[1,8,2048]{2,0,1:T(1,128)S(1)}, u32[]{:S(2)}, u32[]{:S(2)}) async-start(f32[1,8,2048]{2,0,1:T(1,128)} %bitcast.28), calls=%async_computation.5 | async-start | bytes 131072 | tf_op jit(solution)/shard_map/all_to_all | solution.py:132
  108.1 10.2 %all-to-all-start.6 = ((f32[1,8,2048]{2,0,1:T(1,128)}), f32[1,8,2048]{2,0,1:T(1,128)S(1)}, u32[]{:S(2)}, u32[]{:S(2)}) async-start(f32[1,8,2048]{2,0,1:T(1,128)} %bitcast.29), calls=%async_computation.6 | async-start | bytes 131072 | tf_op jit(solution)/shard_map/all_to_all | solution.py:135
  118.3 10.2 %all-to-all-start.7 = ((f32[1,8,2048]{2,0,1:T(1,128)}), f32[1,8,2048]{2,0,1:T(1,128)S(1)}, u32[]{:S(2)}, u32[]{:S(2)}) async-start(f32[1,8,2048]{2,0,1:T(1,128)} %bitcast.32), calls=%async_computation.7 | async-start | bytes 131072 | tf_op jit(solution)/shard_map/all_to_all | solution.py:138
  128.5 10.2 %all-to-all-start.8 = ((f32[1,8,2048]{2,0,1:T(1,128)}), f32[1,8,2048]{2,0,1:T(1,128)S(1)}, u32[]{:S(2)}, u32[]{:S(2)}) async-start(f32[1,8,2048]{2,0,1:T(1,128)} %bitcast.33), calls=%async_computation.8 | async-start | bytes 131072 | tf_op jit(solution)/shard_map/all_to_all | solution.py:141
  138.7 36.4 %all-to-all-start.9 = ((f32[8,1,2048]{2,1,0:T(1,128)}), f32[8,1,2048]{2,1,0:T(1,128)S(1)}, u32[]{:S(2)}, u32[]{:S(2)}) async-start(f32[8,1,2048]{2,1,0:T(1,128)} %copy.23), calls=%async_computation.9 | async-start | bytes 131072 | tf_op jit(solution)/shard_map/all_to_all | solution.py:152
  175.1 10.2 %all-to-all-start.10 = ((f32[8,1,2048]{2,1,0:T(1,128)}), f32[8,1,2048]{2,1,0:T(1,128)S(1)}, u32[]{:S(2)}, u32[]{:S(2)}) async-start(f32[8,1,2048]{2,1,0:T(1,128)} %copy.24), calls=%async_computation.10 | async-start | bytes 131072 | tf_op jit(solution)/shard_map/all_to_all | solution.py:153
where the time goes:
time: 188 us; the launch traced here: 186 us
  starting transfers between devices  68.6 us (36%)
  waiting for transfers between devices  50.7 us (27%)
  blocking collectives  39.4 us (21%)
  other arithmetic  15.4 us (8%)
  local copies, waits for them, and re-layouts  4.78 us (3%)
  between operations  4.42 us (2%)
  matrix products  2.59 us (1%)
    psum x1, blocking collectives, inner_products(): lax.psum((jnp.sum(residual * image), jnp.sum(image * image)), ('tm', 'spa...  30.1 us
    ppermute x7, starting transfers between devices, with_halo(): before = lax.ppermute(last, axis, up)  21.2 us
    all_to_all x1, blocking collectives, on_device(): lax.all_to_all(flat_stiff, 'tm', split_axis=1, concat_axis=0, tiled=True)  9.27 us
    ppermute x7, starting transfers between devices, with_halo(): after = lax.ppermute(first, axis, down)  9.02 us
    all_to_all x1, starting transfers between devices, on_device(): lax.all_to_all(flat_source, 'tm', split_axis=1, concat_axis=0, tiled=True)  7.29 us
    all_to_all x1, waiting for transfers between devices, on_device(): lax.all_to_all(stiff_im.reshape(steps_here, cells), 'tm', split_axis=1, c...  6.59 us
    all_to_all x1, waiting for transfers between devices, on_device(): lax.all_to_all(sol_im.reshape(steps_here, cells), 'tm', split_axis=1, con...  6.59 us
    all_to_all x1, waiting for transfers between devices, on_device(): lax.all_to_all(spec_im, 'tm', split_axis=0, concat_axis=1, tiled=True)  5.89 us
  transfers between devices with their start and end apart: 24, of which 14 were waited for; matrix products, arithmetic and copies ran while one was open for 6% of the time, Pallas kernels for 0%

commit v1 on v0

--- a/solution.py
+++ b/solution.py
@@ -1,8 +1,11 @@
+import functools
 import math
 
 import jax
 import jax.numpy as jnp
 from jax import lax
+from jax.experimental import pallas as pl
+from jax.experimental.pallas import tpu as pltpu
 from jax.sharding import PartitionSpec as P
 
 SWEEPS = 6
@@ -156,6 +159,449 @@
     return (new_iterate, residual_back.reshape(slab_shape))
 
 
+def constants(total):
+    scale = 1.0 / (step_length**frac_order * gamma_factor)
+    power = 1.0 - frac_order
+    b = [(k + 1.0) ** power - float(k) ** power for k in range(total)]
+    d = [scale * (b[k] - (b[k - 1] if k else 0.0)) for k in range(total)]
+    angle = [2.0 * math.pi * i / total for i in range(total)]
+    cos = [math.cos(a) for a in angle]
+    sin = [math.sin(a) for a in angle]
+    half = total // 2
+    lam_re = [sum(d[k] * cos[j * k % total] for k in range(half)) for j in range(total)]
+    lam_im = [-sum(d[k] * sin[j * k % total] for k in range(half)) for j in range(total)]
+    return d, cos, sin, lam_re, lam_im
+
+
+def weighted(terms):
+    result = None
+    for weight, value in terms:
+        if abs(weight) < 1e-9:
+            continue
+        if result is None:
+            result = value if abs(weight - 1.0) < 1e-9 else weight * value
+        elif abs(weight - 1.0) < 1e-9:
+            result = result + value
+        elif abs(weight + 1.0) < 1e-9:
+            result = result - value
+        else:
+            result = result + weight * value
+    return result
+
+
+def pick(index, values):
+    result = jnp.float32(values[0])
+    for i in range(1, len(values)):
+        result = jnp.where(index == i, jnp.float32(values[i]), result)
+    return result
+
+
+def fused_kernel(
+    peers,
+    u_hbm,
+    f_hbm,
+    k_hbm,
+    x_out,
+    r_out,
+    u,
+    f,
+    kap,
+    kap_far,
+    u_halo,
+    wbuf,
+    got_uw,
+    res,
+    spec,
+    got_spec,
+    far_spec,
+    got_res,
+    gain,
+    hop,
+    sol_0,
+    sol_a,
+    sol_b,
+    xy,
+    got_xy,
+    ci,
+    got_ci,
+    part,
+    got_part,
+    load_sem,
+    halo_send,
+    halo_recv,
+    kap_send,
+    kap_recv,
+    uw_send,
+    uw_recv,
+    spec_send,
+    spec_recv,
+    far_send,
+    far_recv,
+    res_send,
+    res_recv,
+    xy_send,
+    xy_recv,
+    ci_send,
+    ci_recv,
+    part_send,
+    part_recv,
+):
+    me = lax.axis_index("tm")
+    side = lax.axis_index("space")
+    ny, nx = u.shape[-2:]
+    reach = SWEEPS
+    low = peers - reach
+    d, cos, sin, lam_re, lam_im = constants(peers)
+    half = peers // 2
+    others = [lax.rem(me + i, peers) for i in range(1, peers)]
+    mesh_type = pl.DeviceIdType.MESH
+
+    def plane(q):
+        return side * (peers - 1) + q * (1 - 2 * side)
+
+    def at_tm(k):
+        return {"tm": k}
+
+    across = {"space": 1 - side}
+
+    def diagonal(k):
+        return {"tm": k, "space": 1 - side}
+
+    def copy(src, dst, send, recv, device):
+        return pltpu.make_async_remote_copy(
+            src_ref=src,
+            dst_ref=dst,
+            send_sem=send,
+            recv_sem=recv,
+            device_id=device,
+            device_id_type=mesh_type,
+        )
+
+    loads = [
+        pltpu.make_async_copy(a, b, load_sem.at[i])
+        for i, (a, b) in enumerate(((u_hbm.at[0], u), (k_hbm, kap), (f_hbm.at[0], f)))
+    ]
+    for load in loads:
+        load.start()
+    barrier = pltpu.get_barrier_semaphore()
+    for k in others:
+        pl.semaphore_signal(barrier, inc=1, device_id=at_tm(k), device_id_type=mesh_type)
+        pl.semaphore_signal(barrier, inc=1, device_id=diagonal(k), device_id_type=mesh_type)
+    pl.semaphore_signal(barrier, inc=1, device_id=across, device_id_type=mesh_type)
+    loads[0].wait()
+    loads[1].wait()
+    loads[2].wait()
+
+    rows = lax.broadcasted_iota(jnp.int32, (ny, nx), 0)
+    lanes = lax.broadcasted_iota(jnp.int32, (ny, nx), 1)
+    not_top = rows > 0
+    not_bottom = rows < ny - 1
+    not_left = lanes > 0
+    not_right = lanes < nx - 1
+
+    def in_plane(v):
+        y = jnp.where(not_top, pltpu.roll(v, 1, 0), 0.0) + jnp.where(
+            not_bottom, pltpu.roll(v, ny - 1, 0), 0.0
+        )
+        x = jnp.where(not_left, pltpu.roll(v, 1, 1), 0.0) + jnp.where(
+            not_right, pltpu.roll(v, nx - 1, 1), 0.0
+        )
+        return y + x
+
+    pl.semaphore_wait(barrier, 2 * peers - 1)
+    halo = copy(u.at[plane(peers - 1)], u_halo, halo_send, halo_recv, across)
+    halo.start()
+    sends = [halo]
+    for k in others:
+        c = copy(
+            u.at[plane(k)], got_uw.at[me, 0], uw_send.at[k, 0], uw_recv.at[me, 0], at_tm(k)
+        )
+        c.start()
+        sends.append(c)
+    kap_copy = copy(kap, kap_far, kap_send, kap_recv, across)
+    kap_copy.start()
+    sends.append(kap_copy)
+
+    def stiff_of_iterate(q, after):
+        value = u[plane(q)]
+        total = in_plane(value) + after
+        if q > 0:
+            total = total + u[plane(q - 1)]
+        wbuf[q] = f[plane(q)] - kap[plane(q)] * (6.0 * value - total)
+
+    for q in range(peers - 1):
+        stiff_of_iterate(q, u[plane(q + 1)])
+    halo.wait_recv()
+    stiff_of_iterate(peers - 1, u_halo[...])
+    for k in others:
+        c = copy(wbuf.at[k], got_uw.at[me, 1], uw_send.at[k, 1], uw_recv.at[me, 1], at_tm(k))
+        c.start()
+        sends.append(c)
+    got_uw[me, 0] = u[plane(me)]
+    got_uw[me, 1] = wbuf[me]
+
+    my_re = pick(me, lam_re)
+    my_im = pick(me, lam_im)
+    kap_copy.wait_recv()
+    depth = peers + reach
+    for q in range(depth):
+        kappa = kap[plane(q)] if q < peers else kap_far[(1 - side) * (peers - 1) + (2 * peers - 1 - q) * (2 * side - 1)]
+        diag = my_re + 6.0 * kappa
+        inverse = 1.0 / (diag * diag + my_im * my_im)
+        g_re = diag * inverse
+        g_im = -my_im * inverse
+        gain[q, 0] = g_re
+        gain[q, 1] = g_im
+        hop[q, 0] = g_re * kappa
+        hop[q, 1] = g_im * kappa
+    zero = jnp.zeros((ny, nx), jnp.float32)
+    for buffer in (sol_0, sol_a, sol_b):
+        buffer[0, 0] = zero
+        buffer[0, 1] = zero
+
+    for k in others:
+        for i in range(2):
+            copy(
+                wbuf.at[k], got_uw.at[k, i], uw_send.at[k, i], uw_recv.at[k, i], at_tm(k)
+            ).wait_recv()
+    residual = []
+    for n in range(peers):
+        history = weighted([(d[n - m], got_uw[m, 0]) for m in range(n + 1)])
+        value = got_uw[n, 1] - history
+        res[n] = value
+        residual.append(value)
+    for j in range(half + 1):
+        real = weighted([(cos[j * n % peers], residual[n]) for n in range(peers)])
+        imag = weighted([(-sin[j * n % peers], residual[n]) for n in range(peers)])
+        if imag is None:
+            imag = zero
+        spec[j, 0] = real
+        spec[j, 1] = imag
+        if 0 < j < half:
+            spec[peers - j, 0] = real
+            spec[peers - j, 1] = -imag
+    for k in others:
+        c = copy(spec.at[k], got_spec.at[me], spec_send.at[k], spec_recv.at[me], at_tm(k))
+        c.start()
+        sends.append(c)
+    got_spec[me] = spec[me]
+
+    def forward(q):
+        return copy(got_spec.at[q], far_spec.at[q], far_send.at[q], far_recv.at[q], across)
+
+    @pl.when(me >= low)
+    def _():
+        copy(spec.at[me], far_spec.at[me], far_send.at[me], far_recv.at[me], across).start()
+
+    for k in others:
+        copy(spec.at[k], got_spec.at[k], spec_send.at[k], spec_recv.at[k], at_tm(k)).wait_recv()
+
+        @pl.when(k >= low)
+        def _():
+            forward(k).start()
+
+    for k in others:
+        c = copy(res.at[k], got_res.at[me], res_send.at[k], res_recv.at[me], at_tm(k))
+        c.start()
+        sends.append(c)
+    got_res[me] = res[me]
+
+    def first_solution(q, s):
+        g_re, g_im = gain[q, 0], gain[q, 1]
+        s_re, s_im = s[0], s[1]
+        sol_0[q + 1, 0] = s_re * g_re - s_im * g_im
+        sol_0[q + 1, 1] = s_re * g_im + s_im * g_re
+
+    for q in range(peers):
+        first_solution(q, got_spec[q])
+    for q in range(low, peers):
+        forward(q).wait_recv()
+    for q in range(peers, depth):
+        first_solution(q, far_spec[2 * peers - 1 - q])
+
+    def neighbours(buffer, q, i):
+        return buffer[q, i] + buffer[q + 2, i] + in_plane(buffer[q + 1, i])
+
+    now = sol_0
+    for sweep in range(SWEEPS - 1):
+        later = sol_b if now is sol_a else sol_a
+
+        def sweep_plane(q, carry, now=now, later=later):
+            n_re = neighbours(now, q, 0)
+            n_im = neighbours(now, q, 1)
+            h_re, h_im = hop[q, 0], hop[q, 1]
+            later[q + 1, 0] = sol_0[q + 1, 0] + (h_re * n_re - h_im * n_im)
+            later[q + 1, 1] = sol_0[q + 1, 1] + (h_re * n_im + h_im * n_re)
+            return carry
+
+        lax.fori_loop(0, depth - 1 - sweep, sweep_plane, 0, unroll=True)
+        now = later
+
+    is_sol = me <= half
+    is_real = jnp.logical_or(me == 0, me == half)
+
+    def stiff_plane(q, carry):
+        kappa = kap[plane(q)]
+        s_re, s_im = now[q + 1, 0], now[q + 1, 1]
+        k_re = kappa * (6.0 * s_re - neighbours(now, q, 0))
+        k_im = kappa * (6.0 * s_im - neighbours(now, q, 1))
+        xy[q, 0] = jnp.where(is_sol, s_re, k_re)
+        xy[q, 1] = jnp.where(is_real, k_re, jnp.where(is_sol, s_im, k_im))
+        return carry
+
+    lax.fori_loop(0, peers, stiff_plane, 0, unroll=True)
+    for k in others:
+        c = copy(xy.at[k], got_xy.at[me], xy_send.at[k], xy_recv.at[me], at_tm(k))
+        c.start()
+        sends.append(c)
+    got_xy[me] = xy[me]
+    for k in others:
+        copy(xy.at[k], got_xy.at[k], xy_send.at[k], xy_recv.at[k], at_tm(k)).wait_recv()
+
+    inv = 1.0 / peers
+    corrections = []
+    for n in range(peers):
+        terms = [(inv, got_xy[0, 0]), (inv * cos[n * half % peers], got_xy[half, 0])]
+        for j in range(1, half):
+            terms.append((2.0 * inv * cos[n * j % peers], got_xy[j, 0]))
+            terms.append((-2.0 * inv * sin[n * j % peers], got_xy[j, 1]))
+        value = weighted(terms)
+        ci[n, 0] = value
+        corrections.append(value)
+    inner_ri = zero
+    inner_ii = zero
+    for n in range(peers):
+        terms = [(inv, got_xy[0, 1]), (inv * cos[n * half % peers], got_xy[half, 1])]
+        for j in range(half + 1, peers):
+            terms.append((2.0 * inv * cos[n * j % peers], got_xy[j, 0]))
+            terms.append((-2.0 * inv * sin[n * j % peers], got_xy[j, 1]))
+        image = weighted(terms + [(d[n - m], corrections[m]) for m in range(n + 1)])
+        ci[n, 1] = image
+        inner_ri = inner_ri + res[n] * image
+        inner_ii = inner_ii + image * image
+    part[0:1] = jnp.sum(inner_ri, axis=0, keepdims=True)
+    part[1:2] = jnp.sum(inner_ii, axis=0, keepdims=True)
+    mine = side * peers + me
+    opposite = (1 - side) * peers
+
+    def part_copy(slot, source, device):
+        return copy(part, got_part.at[source], part_send.at[slot], part_recv.at[source], device)
+
+    for k in others:
+        for slot, device in ((side * peers + k, at_tm(k)), (opposite + k, diagonal(k))):
+            c = part_copy(slot, mine, device)
+            c.start()
+            sends.append(c)
+    c = part_copy(opposite + me, mine, across)
+    c.start()
+    sends.append(c)
+    for k in others:
+        c = copy(ci.at[k], got_ci.at[me], ci_send.at[k], ci_recv.at[me], at_tm(k))
+        c.start()
+        sends.append(c)
+    got_ci[me] = ci[me]
+    got_part[mine] = part[...]
+    for k in others:
+        copy(res.at[k], got_res.at[k], res_send.at[k], res_recv.at[k], at_tm(k)).wait_recv()
+    for k in others:
+        part_copy(side * peers + k, side * peers + k, at_tm(k)).wait_recv()
+        part_copy(opposite + k, opposite + k, diagonal(k)).wait_recv()
+    part_copy(opposite + me, opposite + me, across).wait_recv()
+    sums = got_part[0]
+    for i in range(1, 2 * peers):
+        sums = sums + got_part[i]
+    sums = jnp.sum(sums, axis=1, keepdims=True)
+    step = sums[0:1] / sums[1:2]
+    for k in others:
+        copy(ci.at[k], got_ci.at[k], ci_send.at[k], ci_recv.at[k], at_tm(k)).wait_recv()
+    for q in range(peers):
+        x_out[0, plane(q)] = u[plane(q)] + step * got_ci[q, 0]
+        r_out[0, plane(q)] = got_res[q] - step * got_ci[q, 1]
+    for c in sends:
+        c.wait_send()
+    for q in range(low, peers):
+        forward(q).wait_send()
+
+
+def fused(iterate, source, diffusivity):
+    peers = lax.axis_size("tm")
+    ny, nx = iterate.shape[-2:]
+    depth = peers + SWEEPS
+
+    def buffer(*lead):
+        return pltpu.VMEM(lead + (ny, nx), jnp.float32)
+
+    dma = pltpu.SemaphoreType.DMA
+    shape = jax.ShapeDtypeStruct(iterate.shape, jnp.float32)
+    vmem = pl.BlockSpec(memory_space=pltpu.VMEM)
+    return pl.pallas_call(
+        functools.partial(fused_kernel, peers),
+        out_shape=(shape, shape),
+        in_specs=[pl.BlockSpec(memory_space=pl.ANY)] * 3,
+        out_specs=(vmem, vmem),
+        scratch_shapes=[
+            buffer(peers),
+            buffer(peers),
+            buffer(peers),
+            buffer(peers),
+            buffer(),
+            buffer(peers),
+            buffer(peers, 2),
+            buffer(peers),
+            buffer(peers, 2),
+            buffer(peers, 2),
+            buffer(peers, 2),
+            buffer(peers),
+            buffer(depth, 2),
+            buffer(depth, 2),
+            buffer(depth + 1, 2),
+            buffer(depth + 1, 2),
+            buffer(depth + 1, 2),
+            buffer(peers, 2),
+            buffer(peers, 2),
+            buffer(peers, 2),
+            buffer(peers, 2),
+            pltpu.VMEM((2, nx), jnp.float32),
+            pltpu.VMEM((2 * peers, 2, nx), jnp.float32),
+            dma((3,)),
+            dma,
+            dma,
+            dma,
+            dma,
+            dma((peers, 2)),
+            dma((peers, 2)),
+            dma((peers,)),
+            dma((peers,)),
+            dma((peers,)),
+            dma((peers,)),
+            dma((peers,)),
+            dma((peers,)),
+            dma((peers,)),
+            dma((peers,)),
+            dma((peers,)),
+            dma((peers,)),
+            dma((2 * peers,)),
+            dma((2 * peers,)),
+        ],
+        compiler_params=pltpu.CompilerParams(collective_id=0, has_side_effects=True),
+    )(iterate, source, diffusivity)
+
+
+def on_device_any(iterate, source, diffusivity):
+    steps, planes, ny, nx = iterate.shape
+    peers = lax.axis_size("tm")
+    fits = (
+        steps == 1
+        and planes == peers
+        and peers % 2 == 0
+        and lax.axis_size("space") == 2
+        and planes >= SWEEPS
+        and ny % 8 == 0
+        and nx % 128 == 0
+    )
+    return (fused if fits else on_device)(iterate, source, diffusivity)
+
+
 def solution(mesh):
     in_specs = (
         P(("groups", "tm"), "space", None, None),
@@ -164,5 +610,5 @@
     )
     out_specs = (P(("groups", "tm"), "space", None, None), P(("groups", "tm"), "space", None, None))
     return jax.shard_map(
-        on_device, mesh=mesh, in_specs=in_specs, out_specs=out_specs, check_vma=False
-    )
+        on_device_any, mesh=mesh, in_specs=in_specs, out_specs=out_specs, check_vma=False
+    )

time: 188 us -> 32.6 us (0.17)
  starting transfers between devices: 68.6 us -> 0 us
  waiting for transfers between devices: 50.7 us -> 0 us
  blocking collectives: 39.4 us -> 0 us
  Pallas kernels: 0 us -> 29.6 us
  other arithmetic: 15.4 us -> 0 us
  between operations: 4.42 us -> 0.65 us
  local copies, waits for them, and re-layouts: 4.78 us -> 2.14 us
  matrix products: 2.59 us -> 0 us
    all_to_all x10 -> x0, waiting for transfers between devices: 46.7 us -> none  [the longest x1 6.59 us: on_device(): lax.all_to_all(stiff_im.reshape(steps_here, cells), 'tm', split_axis=1, c...]
    all_to_all x10 -> x0, starting transfers between devices: 38.4 us -> none  [the longest x1 7.29 us: on_device(): lax.all_to_all(flat_source, 'tm', split_axis=1, concat_axis=0, tiled=True)]
    ppermute x14 -> x0, starting transfers between devices: 30.2 us -> none  [the longest x7 21.2 us: with_halo(): before = lax.ppermute(last, axis, up)]
    psum x1 -> x0, blocking collectives: 30.1 us -> none  [inner_products(): lax.psum((jnp.sum(residual * image), jnp.sum(image * image)), ('tm', 'spa...]
    pallas_call x0 -> x1, Pallas kernels: none -> 29.6 us  [fused(): pl.pallas_call(functools.partial(fused_kernel, peers), out_shape=(shape,...]
    all_to_all x1 -> x0, blocking collectives: 9.27 us -> none  [on_device(): lax.all_to_all(flat_stiff, 'tm', split_axis=1, concat_axis=0, tiled=True)]
    add x5 -> x0, other arithmetic: 7.4 us -> none  [the longest x2 3.3 us: jacobi_step(): sol_im + (res_re * inv_im + res_im * inv_re)]
    another operation x14 -> x0, other arithmetic: 4.29 us -> none  [stiffness_pair(): stacked = jnp.stack([sol_re, sol_im])]
  transfers between devices with their start and end apart: 24 -> 0, of which waited for: 14 -> 0; matrix products, arithmetic and copies ran while one was open for 6% -> 0% of each run, Pallas kernels for 0% -> 0%
where the time goes in v1:
time: 32.6 us; the launch traced here: 32.4 us
  Pallas kernels  29.6 us (91%)
  local copies, waits for them, and re-layouts  2.14 us (7%)
  between operations  0.65 us (2%)
    pallas_call x1, Pallas kernels, fused(): pl.pallas_call(functools.partial(fused_kernel, peers), out_shape=(shape,...  29.6 us
    unnamed x4, local copies, waits for them, and re-layouts  2.14 us

profile of v1, /device:TPU:0, one launch (start us, length us, event | category | flops | bytes accessed | tf_op | source)
XLA Modules:
  0.0 32.4 jit_solution(2054136866162926237)
XLA Ops:
  0.6 29.6 %shard_map.50 = (f32[1,8,16,128]{3,2,1,0:T(8,128)}, f32[1,8,16,128]{3,2,1,0:T(8,128)}) custom-call(f32[1,8,16,128]{3,2,1,0:T(8,128)} %u_hbm.1, f32[1,8,16,128]{3,2,1,0:T(8,128)} %f_hbm.1, f32[8,16,128]{2,1,0:T(8,128)} %k_hbm.1), custom_call_target="tpu_custom_call" | custom-call | tf_op jit(solution)/shard_map/pallas_call | solution.py:537
  30.2 0.0 copy-start
  30.2 1.5 %copy.7 = f32[1,8,16,128]{3,2,1,0:T(8,128)} copy(f32[1,8,16,128]{3,2,1,0:T(8,128)} %get-tuple-element.4) | data formatting | bytes 131072
  31.7 0.0 copy-done
  31.7 0.6 %copy.8 = f32[1,8,16,128]{3,2,1,0:T(8,128)} copy(f32[1,8,16,128]{3,2,1,0:T(8,128)S(1)} %copy-done) | data formatting | bytes 131072
Async XLA Ops:
  30.2 1.5 %copy-start = (f32[1,8,16,128]{3,2,1,0:T(8,128)S(1)}, f32[1,8,16,128]{3,2,1,0:T(8,128)}, u32[]{:S(2)}) copy-start(f32[1,8,16,128]{3,2,1,0:T(8,128)} %get-tuple-element.5) | copy-start | bytes 196612

commit v2 on v1

--- a/solution.py
+++ b/solution.py
@@ -196,6 +196,20 @@
     return result
 
 
+def exchange_order(me, peers):
+    if peers & (peers - 1):
+        return [lax.rem(me + i, peers) for i in range(1, peers)]
+    bits = range(peers.bit_length() - 1)
+    result = []
+    for mask in range(peers - 1, 0, -1):
+        partner = 0
+        for b in bits:
+            digit = lax.rem(me // (1 << b), 2)
+            partner = partner + ((1 - digit) if mask >> b & 1 else digit) * (1 << b)
+        result.append(partner)
+    return result
+
+
 def fused_kernel(
     peers,
     u_hbm,
@@ -203,6 +217,7 @@
     k_hbm,
     x_out,
     r_out,
+    dr_out,
     u,
     f,
     kap,
@@ -217,9 +232,7 @@
     got_res,
     gain,
     hop,
-    sol_0,
-    sol_a,
-    sol_b,
+    sols,
     xy,
     got_xy,
     ci,
@@ -253,7 +266,7 @@
     low = peers - reach
     d, cos, sin, lam_re, lam_im = constants(peers)
     half = peers // 2
-    others = [lax.rem(me + i, peers) for i in range(1, peers)]
+    others = exchange_order(me, peers)
     mesh_type = pl.DeviceIdType.MESH
 
     def plane(q):
@@ -286,7 +299,6 @@
     barrier = pltpu.get_barrier_semaphore()
     for k in others:
         pl.semaphore_signal(barrier, inc=1, device_id=at_tm(k), device_id_type=mesh_type)
-        pl.semaphore_signal(barrier, inc=1, device_id=diagonal(k), device_id_type=mesh_type)
     pl.semaphore_signal(barrier, inc=1, device_id=across, device_id_type=mesh_type)
     loads[0].wait()
     loads[1].wait()
@@ -308,7 +320,7 @@
         )
         return y + x
 
-    pl.semaphore_wait(barrier, 2 * peers - 1)
+    pl.semaphore_wait(barrier, peers)
     halo = copy(u.at[plane(peers - 1)], u_halo, halo_send, halo_recv, across)
     halo.start()
     sends = [halo]
@@ -355,9 +367,9 @@
         hop[q, 0] = g_re * kappa
         hop[q, 1] = g_im * kappa
     zero = jnp.zeros((ny, nx), jnp.float32)
-    for buffer in (sol_0, sol_a, sol_b):
-        buffer[0, 0] = zero
-        buffer[0, 1] = zero
+    for level in range(SWEEPS):
+        sols[level, 0, 0] = zero
+        sols[level, 0, 1] = zero
 
     for k in others:
         for i in range(2):
@@ -409,33 +421,37 @@
     def first_solution(q, s):
         g_re, g_im = gain[q, 0], gain[q, 1]
         s_re, s_im = s[0], s[1]
-        sol_0[q + 1, 0] = s_re * g_re - s_im * g_im
-        sol_0[q + 1, 1] = s_re * g_im + s_im * g_re
+        sols[0, q + 1, 0] = s_re * g_re - s_im * g_im
+        sols[0, q + 1, 1] = s_re * g_im + s_im * g_re
+
+    def neighbours(buffer, q, i):
+        return buffer[q, i] + buffer[q + 2, i] + in_plane(buffer[q + 1, i])
+
+    def sweep_plane(level, q):
+        before = sols.at[level - 1]
+        n_re = neighbours(before, q, 0)
+        n_im = neighbours(before, q, 1)
+        h_re, h_im = hop[q, 0], hop[q, 1]
+        sols[level, q + 1, 0] = sols[0, q + 1, 0] + (h_re * n_re - h_im * n_im)
+        sols[level, q + 1, 1] = sols[0, q + 1, 1] + (h_re * n_im + h_im * n_re)
 
     for q in range(peers):
         first_solution(q, got_spec[q])
+    for level in range(1, SWEEPS):
+        lax.fori_loop(0, peers - level, lambda q, c, level=level: sweep_plane(level, q), None, unroll=True)
     for q in range(low, peers):
         forward(q).wait_recv()
     for q in range(peers, depth):
         first_solution(q, far_spec[2 * peers - 1 - q])
-
-    def neighbours(buffer, q, i):
-        return buffer[q, i] + buffer[q + 2, i] + in_plane(buffer[q + 1, i])
-
-    now = sol_0
-    for sweep in range(SWEEPS - 1):
-        later = sol_b if now is sol_a else sol_a
-
-        def sweep_plane(q, carry, now=now, later=later):
-            n_re = neighbours(now, q, 0)
-            n_im = neighbours(now, q, 1)
-            h_re, h_im = hop[q, 0], hop[q, 1]
-            later[q + 1, 0] = sol_0[q + 1, 0] + (h_re * n_re - h_im * n_im)
-            later[q + 1, 1] = sol_0[q + 1, 1] + (h_re * n_im + h_im * n_re)
-            return carry
-
-        lax.fori_loop(0, depth - 1 - sweep, sweep_plane, 0, unroll=True)
-        now = later
+    for level in range(1, SWEEPS):
+        lax.fori_loop(
+            peers - level,
+            depth - level,
+            lambda q, c, level=level: sweep_plane(level, q),
+            None,
+            unroll=True,
+        )
+    now = sols.at[SWEEPS - 1]
 
     is_sol = me <= half
     is_real = jnp.logical_or(me == 0, me == half)
@@ -503,6 +519,8 @@
     got_part[mine] = part[...]
     for k in others:
         copy(res.at[k], got_res.at[k], res_send.at[k], res_recv.at[k], at_tm(k)).wait_recv()
+    for q in range(peers):
+        r_out[0, plane(q)] = got_res[q]
     for k in others:
         part_copy(side * peers + k, side * peers + k, at_tm(k)).wait_recv()
         part_copy(opposite + k, opposite + k, diagonal(k)).wait_recv()
@@ -515,8 +533,8 @@
     for k in others:
         copy(ci.at[k], got_ci.at[k], ci_send.at[k], ci_recv.at[k], at_tm(k)).wait_recv()
     for q in range(peers):
-        x_out[0, plane(q)] = u[plane(q)] + step * got_ci[q, 0]
-        r_out[0, plane(q)] = got_res[q] - step * got_ci[q, 1]
+        x_out[0, plane(q)] = step * got_ci[q, 0]
+        dr_out[0, plane(q)] = step * got_ci[q, 1]
     for c in sends:
         c.wait_send()
     for q in range(low, peers):
@@ -532,13 +550,13 @@
         return pltpu.VMEM(lead + (ny, nx), jnp.float32)
 
     dma = pltpu.SemaphoreType.DMA
-    shape = jax.ShapeDtypeStruct(iterate.shape, jnp.float32)
+    shape = pltpu.VMEM(iterate.shape, jnp.float32)
     vmem = pl.BlockSpec(memory_space=pltpu.VMEM)
-    return pl.pallas_call(
+    update, residual, decrease = pl.pallas_call(
         functools.partial(fused_kernel, peers),
-        out_shape=(shape, shape),
+        out_shape=(shape, shape, shape),
         in_specs=[pl.BlockSpec(memory_space=pl.ANY)] * 3,
-        out_specs=(vmem, vmem),
+        out_specs=(vmem, vmem, vmem),
         scratch_shapes=[
             buffer(peers),
             buffer(peers),
@@ -554,9 +572,7 @@
             buffer(peers),
             buffer(depth, 2),
             buffer(depth, 2),
-            buffer(depth + 1, 2),
-            buffer(depth + 1, 2),
-            buffer(depth + 1, 2),
+            buffer(SWEEPS, depth + 1, 2),
             buffer(peers, 2),
             buffer(peers, 2),
             buffer(peers, 2),
@@ -585,6 +601,7 @@
         ],
         compiler_params=pltpu.CompilerParams(collective_id=0, has_side_effects=True),
     )(iterate, source, diffusivity)
+    return iterate + update, residual - decrease
 
 
 def on_device_any(iterate, source, diffusivity):

time: 32.6 us -> 31.1 us (0.954)
  local copies, waits for them, and re-layouts: 2.14 us -> 0.01 us
  other arithmetic: 0 us -> 1.28 us
  Pallas kernels: 29.6 us -> 28.9 us
    unnamed x4 -> x2, local copies, waits for them, and re-layouts: 2.14 us -> 0.01 us
    pallas_call x1, Pallas kernels: 29.6 us -> 28.9 us  [fused(): pl.pallas_call(functools.partial(fused_kernel, peers), out_shape=(shape,...]
    add x0 -> x1, other arithmetic: none -> 0.64 us  [fused(): return (iterate + update, residual - decrease)]
    sub x0 -> x1, other arithmetic: none -> 0.64 us  [fused(): return (iterate + update, residual - decrease)]
where the time goes in v2:
time: 31.1 us; the launch traced here: 30.9 us
  Pallas kernels  28.9 us (93%)
  other arithmetic  1.28 us (4%)
  between operations  0.65 us (2%)
    pallas_call x1, Pallas kernels, fused(): pl.pallas_call(functools.partial(fused_kernel, peers), out_shape=(shape,...  28.9 us
    add x1, other arithmetic, fused(): return (iterate + update, residual - decrease)  0.64 us
    sub x1, other arithmetic, fused(): return (iterate + update, residual - decrease)  0.64 us

profile of v2, /device:TPU:0, one launch (start us, length us, event | category | flops | bytes accessed | tf_op | source)
XLA Modules:
  0.0 30.9 jit_solution(12501221901241879498)
XLA Ops:
  0.6 0.0 copy-start
  0.6 28.9 %shard_map.50 = (f32[1,8,16,128]{3,2,1,0:T(8,128)S(1)}, f32[1,8,16,128]{3,2,1,0:T(8,128)S(1)}, f32[1,8,16,128]{3,2,1,0:T(8,128)S(1)}) custom-call(f32[1,8,16,128]{3,2,1,0:T(8,128)} %u_hbm.1, f32[1,8,16,128]{3,2,1,0:T(8,128)} %f_hbm.1, f32[8,16,128]{2,1,0:T(8,128)} %k_hbm.1), custom_call_target="tpu_custom_call" | custom-call | tf_op jit(solution)/shard_map/pallas_call | solution.py:555
  29.6 0.0 copy-done
  29.6 0.6 %add.3 = f32[1,8,16,128]{3,2,1,0:T(8,128)} add(f32[1,8,16,128]{3,2,1,0:T(8,128)S(1)} %copy-done, f32[1,8,16,128]{3,2,1,0:T(8,128)S(1)} %get-tuple-element.5) | non-fusion elementwise | flops 16384 | bytes 196608 | tf_op jit(solution)/shard_map/add | solution.py:604
  30.2 0.6 %sub.3 = f32[1,8,16,128]{3,2,1,0:T(8,128)} subtract(f32[1,8,16,128]{3,2,1,0:T(8,128)S(1)} %get-tuple-element.6, f32[1,8,16,128]{3,2,1,0:T(8,128)S(1)} %get-tuple-element.7) | non-fusion elementwise | flops 16384 | bytes 196608 | tf_op jit(solution)/shard_map/sub | solution.py:604
Async XLA Ops:
  0.6 29.0 %copy-start = (f32[1,8,16,128]{3,2,1,0:T(8,128)S(1)}, f32[1,8,16,128]{3,2,1,0:T(8,128)}, u32[]{:S(2)}) copy-start(f32[1,8,16,128]{3,2,1,0:T(8,128)} %u_hbm.1) | copy-start | bytes 196612

commit v3 on v2

--- a/solution.py
+++ b/solution.py
@@ -266,8 +266,17 @@
     low = peers - reach
     d, cos, sin, lam_re, lam_im = constants(peers)
     half = peers // 2
+    start = peers // 4
+
+    def slot_of(k):
+        return lax.rem(k - start + peers, half)
+
+    slot = slot_of(me)
     others = exchange_order(me, peers)
     mesh_type = pl.DeviceIdType.MESH
+
+    def works(k):
+        return jnp.logical_and(k >= start, k < start + half)
 
     def plane(q):
         return side * (peers - 1) + q * (1 - 2 * side)
@@ -352,20 +361,25 @@
     got_uw[me, 0] = u[plane(me)]
     got_uw[me, 1] = wbuf[me]
 
-    my_re = pick(me, lam_re)
-    my_im = pick(me, lam_im)
+    first_lam = pick(slot, lam_re[:half])
+    second_lam = pick(slot, [lam_re[half]] + lam_re[1:half])
+    my_im = pick(slot, [0.0] + lam_im[1:half])
     kap_copy.wait_recv()
     depth = peers + reach
     for q in range(depth):
         kappa = kap[plane(q)] if q < peers else kap_far[(1 - side) * (peers - 1) + (2 * peers - 1 - q) * (2 * side - 1)]
-        diag = my_re + 6.0 * kappa
+        diag = first_lam + 6.0 * kappa
         inverse = 1.0 / (diag * diag + my_im * my_im)
-        g_re = diag * inverse
-        g_im = -my_im * inverse
-        gain[q, 0] = g_re
-        gain[q, 1] = g_im
-        hop[q, 0] = g_re * kappa
-        hop[q, 1] = g_im * kappa
+        other = second_lam + 6.0 * kappa
+        g_first = diag * inverse
+        g_second = other / (other * other + my_im * my_im)
+        g_cross = -my_im * inverse
+        gain[q, 0] = g_first
+        gain[q, 1] = g_second
+        gain[q, 2] = g_cross
+        hop[q, 0] = g_first * kappa
+        hop[q, 1] = g_second * kappa
+        hop[q, 2] = g_cross * kappa
     zero = jnp.zeros((ny, nx), jnp.float32)
     for level in range(SWEEPS):
         sols[level, 0, 0] = zero
@@ -382,47 +396,54 @@
         value = got_uw[n, 1] - history
         res[n] = value
         residual.append(value)
-    for j in range(half + 1):
-        real = weighted([(cos[j * n % peers], residual[n]) for n in range(peers)])
-        imag = weighted([(-sin[j * n % peers], residual[n]) for n in range(peers)])
-        if imag is None:
-            imag = zero
-        spec[j, 0] = real
-        spec[j, 1] = imag
-        if 0 < j < half:
-            spec[peers - j, 0] = real
-            spec[peers - j, 1] = -imag
-    for k in others:
-        c = copy(spec.at[k], got_spec.at[me], spec_send.at[k], spec_recv.at[me], at_tm(k))
-        c.start()
-        sends.append(c)
-    got_spec[me] = spec[me]
+    spec[0, 0] = weighted([(1.0, residual[n]) for n in range(peers)])
+    spec[0, 1] = weighted([(cos[half * n % peers], residual[n]) for n in range(peers)])
+    for j in range(1, half):
+        spec[j, 0] = weighted([(cos[j * n % peers], residual[n]) for n in range(peers)])
+        spec[j, 1] = weighted([(-sin[j * n % peers], residual[n]) for n in range(peers)])
+
+    def spec_copy(k, source):
+        return copy(
+            spec.at[slot_of(k)], got_spec.at[source], spec_send.at[k], spec_recv.at[source], at_tm(k)
+        )
 
     def forward(q):
         return copy(got_spec.at[q], far_spec.at[q], far_send.at[q], far_recv.at[q], across)
 
-    @pl.when(me >= low)
+    for k in others:
+
+        @pl.when(works(k))
+        def _():
+            spec_copy(k, me).start()
+
+    @pl.when(works(me))
     def _():
-        copy(spec.at[me], far_spec.at[me], far_send.at[me], far_recv.at[me], across).start()
-
-    for k in others:
-        copy(spec.at[k], got_spec.at[k], spec_send.at[k], spec_recv.at[k], at_tm(k)).wait_recv()
-
-        @pl.when(k >= low)
+        got_spec[me] = spec[slot]
+
+        @pl.when(me >= low)
         def _():
-            forward(k).start()
+            copy(
+                spec.at[slot], far_spec.at[me], far_send.at[me], far_recv.at[me], across
+            ).start()
+
+        for k in others:
+            copy(
+                spec.at[0], got_spec.at[k], spec_send.at[k], spec_recv.at[k], at_tm(k)
+            ).wait_recv()
+
+            @pl.when(k >= low)
+            def _():
+                forward(k).start()
 
     for k in others:
         c = copy(res.at[k], got_res.at[me], res_send.at[k], res_recv.at[me], at_tm(k))
         c.start()
         sends.append(c)
     got_res[me] = res[me]
-
     def first_solution(q, s):
-        g_re, g_im = gain[q, 0], gain[q, 1]
-        s_re, s_im = s[0], s[1]
-        sols[0, q + 1, 0] = s_re * g_re - s_im * g_im
-        sols[0, q + 1, 1] = s_re * g_im + s_im * g_re
+        cross = gain[q, 2]
+        sols[0, q + 1, 0] = s[0] * gain[q, 0] - s[1] * cross
+        sols[0, q + 1, 1] = s[1] * gain[q, 1] + s[0] * cross
 
     def neighbours(buffer, q, i):
         return buffer[q, i] + buffer[q + 2, i] + in_plane(buffer[q + 1, i])
@@ -431,66 +452,70 @@
         before = sols.at[level - 1]
         n_re = neighbours(before, q, 0)
         n_im = neighbours(before, q, 1)
-        h_re, h_im = hop[q, 0], hop[q, 1]
-        sols[level, q + 1, 0] = sols[0, q + 1, 0] + (h_re * n_re - h_im * n_im)
-        sols[level, q + 1, 1] = sols[0, q + 1, 1] + (h_re * n_im + h_im * n_re)
-
-    for q in range(peers):
-        first_solution(q, got_spec[q])
-    for level in range(1, SWEEPS):
-        lax.fori_loop(0, peers - level, lambda q, c, level=level: sweep_plane(level, q), None, unroll=True)
-    for q in range(low, peers):
-        forward(q).wait_recv()
-    for q in range(peers, depth):
-        first_solution(q, far_spec[2 * peers - 1 - q])
-    for level in range(1, SWEEPS):
-        lax.fori_loop(
-            peers - level,
-            depth - level,
-            lambda q, c, level=level: sweep_plane(level, q),
-            None,
-            unroll=True,
-        )
-    now = sols.at[SWEEPS - 1]
-
-    is_sol = me <= half
-    is_real = jnp.logical_or(me == 0, me == half)
-
-    def stiff_plane(q, carry):
-        kappa = kap[plane(q)]
-        s_re, s_im = now[q + 1, 0], now[q + 1, 1]
-        k_re = kappa * (6.0 * s_re - neighbours(now, q, 0))
-        k_im = kappa * (6.0 * s_im - neighbours(now, q, 1))
-        xy[q, 0] = jnp.where(is_sol, s_re, k_re)
-        xy[q, 1] = jnp.where(is_real, k_re, jnp.where(is_sol, s_im, k_im))
-        return carry
-
-    lax.fori_loop(0, peers, stiff_plane, 0, unroll=True)
-    for k in others:
-        c = copy(xy.at[k], got_xy.at[me], xy_send.at[k], xy_recv.at[me], at_tm(k))
-        c.start()
-        sends.append(c)
-    got_xy[me] = xy[me]
-    for k in others:
-        copy(xy.at[k], got_xy.at[k], xy_send.at[k], xy_recv.at[k], at_tm(k)).wait_recv()
+        cross = hop[q, 2]
+        sols[level, q + 1, 0] = sols[0, q + 1, 0] + (hop[q, 0] * n_re - cross * n_im)
+        sols[level, q + 1, 1] = sols[0, q + 1, 1] + (hop[q, 1] * n_im + cross * n_re)
+
+    def xy_copy(k, source):
+        return copy(xy.at[k], got_xy.at[source], xy_send.at[k], xy_recv.at[source], at_tm(k))
+
+    @pl.when(works(me))
+    def _():
+        for q in range(peers):
+            first_solution(q, got_spec[q])
+        for level in range(1, SWEEPS):
+            lax.fori_loop(0, peers - level, lambda q, c, level=level: sweep_plane(level, q), None, unroll=True)
+        for q in range(low, peers):
+            forward(q).wait_recv()
+        for q in range(peers, depth):
+            first_solution(q, far_spec[2 * peers - 1 - q])
+        for level in range(1, SWEEPS):
+            lax.fori_loop(
+                peers - level,
+                depth - level,
+                lambda q, c, level=level: sweep_plane(level, q),
+                None,
+                unroll=True,
+            )
+        now = sols.at[SWEEPS - 1]
+
+        def stiff_plane(q, carry):
+            kappa = kap[plane(q)]
+            for i in range(2):
+                value = now[q + 1, i]
+                xy[q, i] = value
+                xy[q, 2 + i] = kappa * (6.0 * value - neighbours(now, q, i))
+            return carry
+
+        lax.fori_loop(0, peers, stiff_plane, 0, unroll=True)
+        for k in others:
+            xy_copy(k, slot).start()
+        got_xy[slot] = xy[me]
+
+    for k in others:
+
+        @pl.when(works(k))
+        def _():
+            xy_copy(k, slot_of(k)).wait_recv()
 
     inv = 1.0 / peers
     corrections = []
+
+    def inverse_terms(n, i):
+        terms = [(inv, got_xy[0, i]), (inv * cos[n * half % peers], got_xy[0, i + 1])]
+        for j in range(1, half):
+            terms.append((2.0 * inv * cos[n * j % peers], got_xy[j, i]))
+            terms.append((-2.0 * inv * sin[n * j % peers], got_xy[j, i + 1]))
+        return terms
+
     for n in range(peers):
-        terms = [(inv, got_xy[0, 0]), (inv * cos[n * half % peers], got_xy[half, 0])]
-        for j in range(1, half):
-            terms.append((2.0 * inv * cos[n * j % peers], got_xy[j, 0]))
-            terms.append((-2.0 * inv * sin[n * j % peers], got_xy[j, 1]))
-        value = weighted(terms)
+        value = weighted(inverse_terms(n, 0))
         ci[n, 0] = value
         corrections.append(value)
     inner_ri = zero
     inner_ii = zero
     for n in range(peers):
-        terms = [(inv, got_xy[0, 1]), (inv * cos[n * half % peers], got_xy[half, 1])]
-        for j in range(half + 1, peers):
-            terms.append((2.0 * inv * cos[n * j % peers], got_xy[j, 0]))
-            terms.append((-2.0 * inv * sin[n * j % peers], got_xy[j, 1]))
+        terms = inverse_terms(n, 2)
         image = weighted(terms + [(d[n - m], corrections[m]) for m in range(n + 1)])
         ci[n, 1] = image
         inner_ri = inner_ri + res[n] * image
@@ -504,8 +529,8 @@
         return copy(part, got_part.at[source], part_send.at[slot], part_recv.at[source], device)
 
     for k in others:
-        for slot, device in ((side * peers + k, at_tm(k)), (opposite + k, diagonal(k))):
-            c = part_copy(slot, mine, device)
+        for place, device in ((side * peers + k, at_tm(k)), (opposite + k, diagonal(k))):
+            c = part_copy(place, mine, device)
             c.start()
             sends.append(c)
     c = part_copy(opposite + me, mine, across)
@@ -537,8 +562,18 @@
         dr_out[0, plane(q)] = step * got_ci[q, 1]
     for c in sends:
         c.wait_send()
-    for q in range(low, peers):
-        forward(q).wait_send()
+    for k in others:
+
+        @pl.when(works(k))
+        def _():
+            spec_copy(k, me).wait_send()
+
+    @pl.when(works(me))
+    def _():
+        for q in range(low, peers):
+            forward(q).wait_send()
+        for k in others:
+            xy_copy(k, slot).wait_send()
 
 
 def fused(iterate, source, diffusivity):
@@ -566,15 +601,15 @@
             buffer(peers),
             buffer(peers, 2),
             buffer(peers),
-            buffer(peers, 2),
+            buffer(peers // 2, 2),
             buffer(peers, 2),
             buffer(peers, 2),
             buffer(peers),
-            buffer(depth, 2),
-            buffer(depth, 2),
+            buffer(depth, 3),
+            buffer(depth, 3),
             buffer(SWEEPS, depth + 1, 2),
-            buffer(peers, 2),
-            buffer(peers, 2),
+            buffer(peers, 4),
+            buffer(peers // 2, 4),
             buffer(peers, 2),
             buffer(peers, 2),
             pltpu.VMEM((2, nx), jnp.float32),
@@ -610,7 +645,7 @@
     fits = (
         steps == 1
         and planes == peers
-        and peers % 2 == 0
+        and peers % 4 == 0
         and lax.axis_size("space") == 2
         and planes >= SWEEPS
         and ny % 8 == 0

time: 31.1 us -> 29.3 us (0.942)
  Pallas kernels: 28.9 us -> 27.2 us
    pallas_call x1, Pallas kernels: 28.9 us -> 27.2 us  [fused(): pl.pallas_call(functools.partial(fused_kernel, peers), out_shape=(shape,...]
where the time goes in v3:
time: 29.3 us; the launch traced here: 29.2 us
  Pallas kernels  27.2 us (93%)
  other arithmetic  1.28 us (4%)
  between operations  0.65 us (2%)
    pallas_call x1, Pallas kernels, fused(): pl.pallas_call(functools.partial(fused_kernel, peers), out_shape=(shape,...  27.2 us
    add x1, other arithmetic, fused(): return (iterate + update, residual - decrease)  0.64 us
    sub x1, other arithmetic, fused(): return (iterate + update, residual - decrease)  0.64 us

profile of v3, /device:TPU:0, one launch (start us, length us, event | category | flops | bytes accessed | tf_op | source)
XLA Modules:
  0.0 29.2 jit_solution(10275265357499804464)
XLA Ops:
  0.6 0.0 copy-start
  0.6 27.2 %shard_map.50 = (f32[1,8,16,128]{3,2,1,0:T(8,128)S(1)}, f32[1,8,16,128]{3,2,1,0:T(8,128)S(1)}, f32[1,8,16,128]{3,2,1,0:T(8,128)S(1)}) custom-call(f32[1,8,16,128]{3,2,1,0:T(8,128)} %u_hbm.1, f32[1,8,16,128]{3,2,1,0:T(8,128)} %f_hbm.1, f32[8,16,128]{2,1,0:T(8,128)} %k_hbm.1), custom_call_target="tpu_custom_call" | custom-call | tf_op jit(solution)/shard_map/pallas_call | solution.py:590
  27.9 0.0 copy-done
  27.9 0.6 %add.3 = f32[1,8,16,128]{3,2,1,0:T(8,128)} add(f32[1,8,16,128]{3,2,1,0:T(8,128)S(1)} %copy-done, f32[1,8,16,128]{3,2,1,0:T(8,128)S(1)} %get-tuple-element.5) | non-fusion elementwise | flops 16384 | bytes 196608 | tf_op jit(solution)/shard_map/add | solution.py:639
  28.5 0.6 %sub.3 = f32[1,8,16,128]{3,2,1,0:T(8,128)} subtract(f32[1,8,16,128]{3,2,1,0:T(8,128)S(1)} %get-tuple-element.6, f32[1,8,16,128]{3,2,1,0:T(8,128)S(1)} %get-tuple-element.7) | non-fusion elementwise | flops 16384 | bytes 196608 | tf_op jit(solution)/shard_map/sub | solution.py:639
Async XLA Ops:
  0.6 27.2 %copy-start = (f32[1,8,16,128]{3,2,1,0:T(8,128)S(1)}, f32[1,8,16,128]{3,2,1,0:T(8,128)}, u32[]{:S(2)}) copy-start(f32[1,8,16,128]{3,2,1,0:T(8,128)} %u_hbm.1) | copy-start | bytes 196612
